TPU v7x, 32 devices: a whole 2x2x4 slice. The times are simulated.
32 devices in a mesh: slab: 16 (over z, y, x), comp: 2 (over core).
Axes of the slice: x: 2, y: 2, z: 4, core: 2. Of those that a mesh axis runs over, the one named last changes fastest.
Arguments:
- polarization: float32 [6, 16, 128, 128], P('comp', 'slab'), parts along dimension 0, may hold values from -6 to 6
- inverse_polarizability: float32 [16, 128, 128], P('slab'), may hold values from 0.5 to 2
- occupancy: int32 [16, 16, 16], P('slab'), may hold values 0 or 1
- green_fourier: float32 [6, 256, 32, 256], P(None, 'slab'), may hold values from -12 to 12
Outputs:
- first_image: float32 [6, 16, 128, 128], P('comp', 'slab'), parts along dimension 0
- second_image: float32 [6, 16, 128, 128], P('comp', 'slab'), parts along dimension 0
There are 2 independent parts, one for each index of `comp`. A program takes and returns all parts, laid end to end along the dimension named above; an argument that names none is the same for every part. Nothing has to cross between parts.
All inputs are finite; a program needn't handle non-finite values. No bound on the sum of `occupancy` on one device may be relied on, other than what follows from the above.
Results may differ from a plain program's by a relative error of at most 0.0001.
Values sent between devices are 32-bit elements; how exact they have to be, the bound alone decides.
A program may use at most 64 MiB of HBM per device.

v0:
```python
import functools
import math

import jax
import jax.numpy as jnp
import numpy as np
from jax import lax
from jax.experimental import pallas as pl
from jax.experimental.pallas import tpu as pltpu
from jax.sharding import PartitionSpec as P

BLOCK = 8
MATVECS = 2
F32 = jnp.float32
BF16 = jnp.bfloat16
COMBOS = ((0, 3, 4), (3, 1, 5), (4, 5, 2))


def tables(count_in, count_out, length):
    phase = np.arange(count_in)[:, None] * np.arange(count_out)[None, :] % length
    angle = phase * (2.0 * math.pi / length)
    return np.cos(angle), np.sin(angle)


def split_table(table):
    table = table.astype(np.float32)
    high = table.astype(jnp.bfloat16)
    low = (table - high.astype(np.float32)).astype(jnp.bfloat16)
    return high, low


def split(value):
    high = value.astype(BF16)
    return high, (value - high.astype(F32)).astype(BF16)


def twiddle(re, im, num, length, sign):
    num = num * sign % length
    if num == 0:
        return re, im
    if 4 * num == length:
        return -im, re
    if 2 * num == length:
        return -re, -im
    if 4 * num == 3 * length:
        return im, -re
    c = math.cos(2.0 * math.pi * num / length)
    s = math.sin(2.0 * math.pi * num / length)
    if (8 * num) % length == 0:
        a = abs(c)
        p, m = (re + im) * a, (re - im) * a
        return {1: (m, p), 3: (-p, m), 5: (-m, -p), 7: (p, -m)}[8 * num // length]
    return re * c - im * s, re * s + im * c


def fft(values, sign):
    n = len(values)
    if n == 1:
        return values
    even, odd = fft(values[0::2], sign), fft(values[1::2], sign)
    low, high = [], []
    for k in range(n // 2):
        (er, ei), (o_r, oi) = even[k], twiddle(*odd[k], k, n, sign)
        low.append((er + o_r, ei + oi))
        high.append((er - o_r, ei - oi))
    return low + high


def three_pass(pair, table_pair, dims):
    dot = functools.partial(lax.dot_general, dimension_numbers=dims, preferred_element_type=F32)
    (vh, vl), (th, tl) = pair, table_pair
    return dot(vh, th) + (dot(vl, th) + dot(vh, tl))


def kernel(
    n, cells_x, padded_x, kz_own, kc,
    pol_ref, inv_ref, occ_ref, green_ref, wz_h, wz_l, wy_h, wy_l, vy_h, vy_l, vz_h, vz_l,
    first_ref, second_ref,
    green_raw, green, mask_ref, raw_out, raw_in, out_t, in_t, lines, spec, out_u, in_u, part_out, part_in,
    green_sem, ws_sem, wr_sem, ts_sem, tr_sem, cs_sem, cr_sem, os_sem, or_sem, ps_sem, pr_sem,
):
    me = lax.axis_index("slab")
    group = n // 2
    here = me // group
    seat = lax.rem(me, group)
    twin = lax.rem(me + group, n)
    base = here * group
    chunks = kz_own // kc
    cells_y, cells_z = mask_ref.shape
    padded_y = 2 * cells_y
    halves = padded_y // 128
    kz_half = group * kz_own
    green_copy = pltpu.make_async_copy(green_ref, green_raw, green_sem)
    green_copy.start()

    def signal(device):
        pl.semaphore_signal(barrier, inc=1, device_id={"slab": device}, device_id_type=pl.DeviceIdType.MESH)

    def remote(source, target, send_sem, recv_sem, device):
        return pltpu.make_async_remote_copy(
            src_ref=source, dst_ref=target, send_sem=send_sem, recv_sem=recv_sem,
            device_id={"slab": device}, device_id_type=pl.DeviceIdType.MESH,
        )

    barrier = pltpu.get_barrier_semaphore()
    signal(twin)

    def greet(k, carry):
        signal(base + lax.rem(seat + k, group))
        return carry

    lax.fori_loop(1, group, greet, 0)

    blocks_y, blocks_z = occ_ref.shape[1:]
    up_y = lax.broadcasted_iota(jnp.int32, (cells_y, blocks_y), 0) // BLOCK
    up_y = (up_y == lax.broadcasted_iota(jnp.int32, (cells_y, blocks_y), 1)).astype(F32).astype(BF16)
    up_z = lax.broadcasted_iota(jnp.int32, (blocks_z, cells_z), 1) // BLOCK
    up_z = (up_z == lax.broadcasted_iota(jnp.int32, (blocks_z, cells_z), 0)).astype(F32).astype(BF16)
    flags = occ_ref[0].astype(F32).astype(BF16)
    spread = jnp.dot(up_y, flags, preferred_element_type=F32).astype(BF16)
    mask_ref[...] = jnp.dot(spread, up_z, preferred_element_type=F32)

    def order_green():
        green_copy.wait()

        def one(g, carry):
            for j in range(chunks):
                for t in range(0, padded_x, 8):
                    tile = green_raw[g, j * kc:(j + 1) * kc, t:t + 8, :]
                    tile = jnp.swapaxes(tile, 0, 1)
                    for h in range(halves):
                        green[j * halves + h, g, t:t + 8] = tile[:, :, h * 128:(h + 1) * 128]
            return carry

        lax.fori_loop(0, 6, one, 0)

    def send_raw(step, c, field):
        raw_out[c] = field
        remote(raw_out.at[c], raw_in.at[c], ws_sem.at[step, c], wr_sem.at[step, c], twin).start()

    def forward_z(step, c, which, field):
        pair = split(field)
        slab = me if which == 0 else twin
        for part in range(2):
            dims = (((1,), (1,)), ((), ()))
            res = three_pass((wz_h[here, part], wz_l[here, part]), pair, dims)
            out_t[c, which, :, part] = res.reshape(group, kz_own, cells_y)

        def send(k, carry):
            to = lax.rem(seat + k, group)
            remote(
                out_t.at[c, which, to], in_t.at[c, slab], ts_sem.at[step, c], tr_sem.at[step, c], base + to
            ).start()
            return carry

        lax.fori_loop(1, group, send, 0)
        in_t[c, slab] = out_t[c, which, seat]

    def drain(view, sem):
        pltpu.make_async_copy(view, view, sem).wait()

    def forward_yx(step, c):
        drain(in_t.at[c, pl.ds(0, n - 2)], tr_sem.at[step, c])
        parts = [in_t[c, :, part].reshape(cells_x * kz_own, cells_y) for part in range(2)]
        dims = (((1,), (0,)), ((), ()))
        res = three_pass(split(jnp.concatenate(parts, axis=1)), (wy_h[...], wy_l[...]), dims)
        for part in range(2):
            for h in range(halves):
                at = part * padded_y + h * 128
                piece = res[:, at:at + 128].reshape(cells_x, kz_own, 128)
                for j in range(chunks):
                    lines[j * halves + h, part] = piece[:, j * kc:(j + 1) * kc]

        def columns(i, carry):
            line = [(lines[i, 0, x], lines[i, 1, x]) for x in range(cells_x)]
            for m, (re, im) in enumerate(fft(line, -1)):
                spec[i, 2 * c, 2 * m], spec[i, 2 * c + 1, 2 * m] = re, im
            line = [twiddle(lines[i, 0, x], lines[i, 1, x], x, padded_x, -1) for x in range(cells_x)]
            for m, (re, im) in enumerate(fft(line, -1)):
                spec[i, 2 * c, 2 * m + 1], spec[i, 2 * c + 1, 2 * m + 1] = re, im
            return carry

        lax.fori_loop(0, chunks * halves, columns, 0)

    def backward_xy(step, a):
        row = COMBOS[a]

        def columns(i, carry):
            def field(k):
                g = [green[i, r, k] for r in row]
                s = [spec[i, r, k] for r in range(6)]
                return g[0] * s[0] + g[1] * s[2] + g[2] * s[4], g[0] * s[1] + g[1] * s[3] + g[2] * s[5]

            even = fft([field(k) for k in range(0, padded_x, 2)], 1)
            for x in range(cells_x):
                lines[i, 0, x], lines[i, 1, x] = even[x]
            odd = fft([field(k) for k in range(1, padded_x, 2)], 1)
            for x in range(cells_x):
                re, im = twiddle(*odd[x], x, padded_x, 1)
                lines[i, 0, x] += re
                lines[i, 1, x] += im
            return carry

        lax.fori_loop(0, chunks * halves, columns, 0)
        parts = []
        for part in range(2):
            for h in range(halves):
                pieces = [lines[j * halves + h, part] for j in range(chunks)]
                piece = pieces[0] if chunks == 1 else jnp.concatenate(pieces, axis=1)
                parts.append(piece.reshape(cells_x * kz_own, 128))
        dims = (((1,), (0,)), ((), ()))
        res = three_pass(split(jnp.concatenate(parts, axis=1)), (vy_h[...], vy_l[...]), dims)
        for part in range(2):
            piece = res[:, part * cells_y:(part + 1) * cells_y]
            out_u[a, :, part] = piece.reshape(cells_x, kz_own, cells_y)
        send_back(step, a, 1, (1 - here) * group, cs_sem, cr_sem)
        send_back(step, a, 0, base, os_sem, or_sem)

    def send_back(step, a, which, first, s_sem, r_sem):
        def send(k, carry):
            to = lax.rem(seat + k, group)
            remote(
                out_u.at[a, first + to], in_u.at[a, which, seat], s_sem.at[step, a], r_sem.at[step, a], base + to
            ).start()
            return carry

        lax.fori_loop(1, group, send, 0)
        in_u[a, which, seat] = out_u[a, first + seat]

    def inverse_z(a, which):
        total = None
        for part in range(2):
            field = in_u[a, which, :, part].reshape(kz_half, cells_y)
            dims = (((0,), (0,)), ((), ()))
            term = three_pass(split(field), (vz_h[here, part], vz_l[here, part]), dims)
            total = term if total is None else total + term
        return total

    def send_part(step, a):
        drain(in_u.at[a, 1, pl.ds(0, group - 1)], cr_sem.at[step, a])
        part_out[a] = inverse_z(a, 1)
        remote(part_out.at[a], part_in.at[a], ps_sem.at[step, a], pr_sem.at[step, a], twin).start()

    for step in range(MATVECS):
        source, image = (pol_ref, first_ref) if step == 0 else (first_ref, second_ref)
        if step == 0:
            pl.semaphore_wait(barrier, group)
            for c in range(3):
                send_raw(step, c, source[c, 0] * mask_ref[...])
            for c in range(3):
                forward_z(step, c, 0, raw_out[c])
            order_green()
        for c in range(3):
            drain(raw_in.at[c], wr_sem.at[step, c])
            forward_z(step, c, 1, raw_in[c])
            if c > 0:
                forward_yx(step, c - 1)
        forward_yx(step, 2)
        for a in range(3):
            backward_xy(step, a)
            if a > 0:
                send_part(step, a - 1)
        send_part(step, 2)
        for c in range(3):
            drain(raw_out.at[c], ws_sem.at[step, c])
            drain(in_t.at[c, pl.ds(0, n - 2)], ts_sem.at[step, c])
        for a in range(3):
            drain(in_u.at[a, 0, pl.ds(0, group - 1)], or_sem.at[step, a])
            own = inverse_z(a, 0)
            masked = source[a, 0] * mask_ref[...]
            drain(part_in.at[a], pr_sem.at[step, a])
            image[a, 0] = inv_ref[0] * masked - mask_ref[...] * (own + part_in[a])
            if step + 1 < MATVECS:
                send_raw(step + 1, a, image[a, 0] * mask_ref[...])
                forward_z(step + 1, a, 0, raw_out[a])
        for a in range(3):
            drain(in_u.at[a, 1, pl.ds(0, group - 1)], cs_sem.at[step, a])
            drain(in_u.at[a, 0, pl.ds(0, group - 1)], os_sem.at[step, a])
            drain(part_out.at[a], ps_sem.at[step, a])


def deliver(first_ref, second_ref, first_out, second_out, first, second, in_sem, out_sem):
    loads = [
        pltpu.make_async_copy(source, held, in_sem.at[i])
        for i, (source, held) in enumerate(((first_ref, first), (second_ref, second)))
    ]
    stores = [
        pltpu.make_async_copy(held, target, out_sem.at[i])
        for i, (held, target) in enumerate(((first, first_out), (second, second_out)))
    ]
    for copy in loads:
        copy.start()
    for load, store in zip(loads, stores):
        load.wait()
        store.start()
    for store in stores:
        store.wait()


def per_device(n, polarization, inverse_polarizability, occupancy, green_fourier):
    _, _, cells_y, cells_z = polarization.shape
    _, kz_own, padded_x, padded_y = green_fourier.shape
    padded_z = 2 * cells_z
    cells_x = padded_x // 2
    kc = min(8, kz_own)
    chunks = kz_own // kc
    halves = padded_y // 128
    cos, sin = tables(padded_z, cells_z, padded_z)
    wz = split_table(np.stack([cos, -sin]).reshape(2, 2, cells_z, cells_z).swapaxes(0, 1))
    cos, sin = tables(cells_y, padded_y, padded_y)
    wy = split_table(np.block([[cos, -sin], [sin, cos]]))
    cos, sin = tables(padded_y, cells_y, padded_y)
    vy = split_table(np.block([[cos, sin], [-sin, cos]]))
    cos, sin = tables(padded_z, cells_z, padded_z)
    vz = np.stack([cos, -sin]).reshape(2, 2, cells_z, cells_z).swapaxes(0, 1)
    vz = split_table(vz / (padded_x * padded_y * padded_z))
    vmem = pl.BlockSpec(memory_space=pltpu.VMEM)
    images = pl.pallas_call(
        functools.partial(kernel, n, cells_x, padded_x, kz_own, kc),
        out_shape=(jax.ShapeDtypeStruct(polarization.shape, F32),) * 2,
        in_specs=[vmem] * 3 + [pl.BlockSpec(memory_space=pl.ANY)] + [vmem] * 8,
        out_specs=(vmem, vmem),
        scratch_shapes=[
            pltpu.VMEM(green_fourier.shape, F32),
            pltpu.VMEM((chunks * halves, 6, padded_x, kc, 128), F32),
            pltpu.VMEM((cells_y, cells_z), F32),
            pltpu.VMEM((3, cells_y, cells_z), F32),
            pltpu.VMEM((3, cells_y, cells_z), F32),
            pltpu.VMEM((3, 2, n // 2, 2, kz_own, cells_y), F32),
            pltpu.VMEM((3, n, 2, kz_own, cells_y), F32),
            pltpu.VMEM((chunks * halves, 2, cells_x, kc, 128), F32),
            pltpu.VMEM((chunks * halves, 6, padded_x, kc, 128), F32),
            pltpu.VMEM((3, n, 2, kz_own, cells_y), F32),
            pltpu.VMEM((3, 2, n // 2, 2, kz_own, cells_y), F32),
            pltpu.VMEM((3, cells_y, cells_z), F32),
            pltpu.VMEM((3, cells_y, cells_z), F32),
            pltpu.SemaphoreType.DMA,
            *[pltpu.SemaphoreType.DMA((MATVECS, 3))] * 10,
        ],
        compiler_params=pltpu.CompilerParams(
            collective_id=0, has_side_effects=True, vmem_limit_bytes=60 * 1024 * 1024
        ),
    )(polarization, inverse_polarizability, occupancy, green_fourier, *map(jnp.asarray, wz + wy + vy + vz))
    anywhere = pl.BlockSpec(memory_space=pl.ANY)
    return pl.pallas_call(
        deliver,
        out_shape=(jax.ShapeDtypeStruct(polarization.shape, F32),) * 2,
        in_specs=[anywhere] * 2,
        out_specs=(anywhere, anywhere),
        scratch_shapes=[pltpu.VMEM(polarization.shape, F32)] * 2 + [pltpu.SemaphoreType.DMA((2,))] * 2,
    )(*images)


def solution(mesh):
    return jax.shard_map(
        functools.partial(per_device, mesh.shape["slab"]),
        mesh=mesh,
        in_specs=(
            P("comp", "slab", None, None),
            P("slab", None, None),
            P("slab", None, None),
            P(None, "slab", None, None),
        ),
        out_specs=(P("comp", "slab", None, None), P("comp", "slab", None, None)),
        check_vma=False,
    )
```

profile of v0, /device:TPU:0, one launch (start us, length us, event | category | flops | bytes accessed | tf_op | source)
XLA Modules:
  0.0 76.3 jit_solution(289845532816997189)
XLA Ops:
  0.6 73.9 %shard_map.131 = (f32[3,1,128,128]{3,2,1,0:T(8,128)}, f32[3,1,128,128]{3,2,1,0:T(8,128)}) custom-call(f32[3,1,128,128]{3,2,1,0:T(8,128)} %pol_ref.1, f32[1,128,128]{2,1,0:T(8,128)} %inv_ref.1, s32[1,16,16]{2,1,0:T(8,128)} %occ_ref.1, f32[6,16,32,256]{3,2,1,0:T(8,128)} %green_ref.1, bf16[2,2,128,128]{3,2,1,0:T(8,128)(2,1)} %constant.16.clone.wz_h, ...), custom_call_target="tpu_custom_call" | custom-call | tf_op jit(solution)/shard_map/pallas_call | solution.py:318
  74.6 1.7 %shard_map.132 = (f32[3,1,128,128]{3,2,1,0:T(8,128)}, f32[3,1,128,128]{3,2,1,0:T(8,128)}) custom-call(f32[3,1,128,128]{3,2,1,0:T(8,128)} %get-tuple-element.4.first_ref, f32[3,1,128,128]{3,2,1,0:T(8,128)} %get-tuple-element.5.second_ref), custom_call_target="tpu_custom_call" | custom-call | tf_op jit(solution)/shard_map/pallas_call | solution.py:345
where the time goes:
time: 76.5 us; the launch traced here: 76.3 us
  Pallas kernels  75.7 us (99%)
    pallas_call x1, Pallas kernels, per_device(): pl.pallas_call(functools.partial(kernel, n, cells_x, padded_x, kz_own, kc...  73.9 us
    pallas_call x1, Pallas kernels, per_device(): pl.pallas_call(deliver, out_shape=(jax.ShapeDtypeStruct(polarization.shap...  1.73 us

commit v1 on v0

--- a/solution.py
+++ b/solution.py
@@ -74,11 +74,16 @@
 
 def kernel(
     n, cells_x, padded_x, kz_own, kc,
-    pol_ref, inv_ref, occ_ref, green_ref, wz_h, wz_l, wy_h, wy_l, vy_h, vy_l, vz_h, vz_l,
-    first_ref, second_ref,
-    green_raw, green, mask_ref, raw_out, raw_in, out_t, in_t, lines, spec, out_u, in_u, part_out, part_in,
-    green_sem, ws_sem, wr_sem, ts_sem, tr_sem, cs_sem, cr_sem, os_sem, or_sem, ps_sem, pr_sem,
+    pol_hbm, inv_hbm, occ_hbm, green_ref, *refs,
 ):
+    tables_hbm, refs = refs[:8], refs[8:]
+    first_ref, second_ref, pol_ref, inv_ref, occ_ref, *refs = refs
+    tables_vmem, refs = refs[:8], refs[8:]
+    wz_h, wz_l, wy_h, wy_l, vy_h, vy_l, vz_h, vz_l = tables_vmem
+    (
+        green_raw, green, mask_ref, raw_out, raw_in, out_t, in_t, lines, spec, out_u, in_u, part_out, part_in,
+        green_sem, load_sem, ws_sem, wr_sem, ts_sem, tr_sem, cs_sem, cr_sem, os_sem, or_sem, ps_sem, pr_sem,
+    ) = refs
     me = lax.axis_index("slab")
     group = n // 2
     here = me // group
@@ -89,9 +94,6 @@
     cells_y, cells_z = mask_ref.shape
     padded_y = 2 * cells_y
     halves = padded_y // 128
-    kz_half = group * kz_own
-    green_copy = pltpu.make_async_copy(green_ref, green_raw, green_sem)
-    green_copy.start()
 
     def signal(device):
         pl.semaphore_signal(barrier, inc=1, device_id={"slab": device}, device_id_type=pl.DeviceIdType.MESH)
@@ -110,6 +112,16 @@
         return carry
 
     lax.fori_loop(1, group, greet, 0)
+    sources = (occ_hbm, pol_hbm, inv_hbm, *tables_hbm)
+    targets = (occ_ref, pol_ref, inv_ref, *tables_vmem)
+    loads = [
+        pltpu.make_async_copy(source, target, load_sem.at[i]) for i, (source, target) in enumerate(zip(sources, targets))
+    ]
+    for load in loads:
+        load.start()
+    green_copy = pltpu.make_async_copy(green_ref, green_raw, green_sem)
+    green_copy.start()
+    loads[0].wait()
 
     blocks_y, blocks_z = occ_ref.shape[1:]
     up_y = lax.broadcasted_iota(jnp.int32, (cells_y, blocks_y), 0) // BLOCK
@@ -138,40 +150,39 @@
         raw_out[c] = field
         remote(raw_out.at[c], raw_in.at[c], ws_sem.at[step, c], wr_sem.at[step, c], twin).start()
 
-    def forward_z(step, c, which, field):
-        pair = split(field)
+    def forward_z(c, which, field):
+        dims = (((1,), (1,)), ((), ()))
+        res = three_pass((wz_h[here], wz_l[here]), split(field), dims)
+        out_t[c, which] = res.reshape(chunks, group, 2, kc, cells_y)
+
+    def send_block(step, c, which, j):
         slab = me if which == 0 else twin
-        for part in range(2):
-            dims = (((1,), (1,)), ((), ()))
-            res = three_pass((wz_h[here, part], wz_l[here, part]), pair, dims)
-            out_t[c, which, :, part] = res.reshape(group, kz_own, cells_y)
 
         def send(k, carry):
             to = lax.rem(seat + k, group)
             remote(
-                out_t.at[c, which, to], in_t.at[c, slab], ts_sem.at[step, c], tr_sem.at[step, c], base + to
+                out_t.at[c, which, j, to], in_t.at[c, j, slab], ts_sem.at[step, c, j], tr_sem.at[step, c, j], base + to
             ).start()
             return carry
 
         lax.fori_loop(1, group, send, 0)
-        in_t[c, slab] = out_t[c, which, seat]
+        in_t[c, j, slab] = out_t[c, which, j, seat]
 
     def drain(view, sem):
         pltpu.make_async_copy(view, view, sem).wait()
 
-    def forward_yx(step, c):
-        drain(in_t.at[c, pl.ds(0, n - 2)], tr_sem.at[step, c])
-        parts = [in_t[c, :, part].reshape(cells_x * kz_own, cells_y) for part in range(2)]
+    def forward_yx(step, c, j):
+        drain(in_t.at[c, j, pl.ds(0, n - 2)], tr_sem.at[step, c, j])
+        parts = [in_t[c, j, :, part].reshape(cells_x * kc, cells_y) for part in range(2)]
         dims = (((1,), (0,)), ((), ()))
         res = three_pass(split(jnp.concatenate(parts, axis=1)), (wy_h[...], wy_l[...]), dims)
         for part in range(2):
             for h in range(halves):
                 at = part * padded_y + h * 128
-                piece = res[:, at:at + 128].reshape(cells_x, kz_own, 128)
-                for j in range(chunks):
-                    lines[j * halves + h, part] = piece[:, j * kc:(j + 1) * kc]
-
-        def columns(i, carry):
+                lines[j * halves + h, part] = res[:, at:at + 128].reshape(cells_x, kc, 128)
+
+        def columns(h, carry):
+            i = j * halves + h
             line = [(lines[i, 0, x], lines[i, 1, x]) for x in range(cells_x)]
             for m, (re, im) in enumerate(fft(line, -1)):
                 spec[i, 2 * c, 2 * m], spec[i, 2 * c + 1, 2 * m] = re, im
@@ -180,12 +191,14 @@
                 spec[i, 2 * c, 2 * m + 1], spec[i, 2 * c + 1, 2 * m + 1] = re, im
             return carry
 
-        lax.fori_loop(0, chunks * halves, columns, 0)
-
-    def backward_xy(step, a):
+        lax.fori_loop(0, halves, columns, 0)
+
+    def backward_xy(step, a, j):
         row = COMBOS[a]
 
-        def columns(i, carry):
+        def columns(h, carry):
+            i = j * halves + h
+
             def field(k):
                 g = [green[i, r, k] for r in row]
                 s = [spec[i, r, k] for r in range(6)]
@@ -201,81 +214,91 @@
                 lines[i, 1, x] += im
             return carry
 
-        lax.fori_loop(0, chunks * halves, columns, 0)
-        parts = []
-        for part in range(2):
-            for h in range(halves):
-                pieces = [lines[j * halves + h, part] for j in range(chunks)]
-                piece = pieces[0] if chunks == 1 else jnp.concatenate(pieces, axis=1)
-                parts.append(piece.reshape(cells_x * kz_own, 128))
+        lax.fori_loop(0, halves, columns, 0)
+        parts = [
+            lines[j * halves + h, part].reshape(cells_x * kc, 128) for part in range(2) for h in range(halves)
+        ]
         dims = (((1,), (0,)), ((), ()))
         res = three_pass(split(jnp.concatenate(parts, axis=1)), (vy_h[...], vy_l[...]), dims)
         for part in range(2):
             piece = res[:, part * cells_y:(part + 1) * cells_y]
-            out_u[a, :, part] = piece.reshape(cells_x, kz_own, cells_y)
-        send_back(step, a, 1, (1 - here) * group, cs_sem, cr_sem)
-        send_back(step, a, 0, base, os_sem, or_sem)
-
-    def send_back(step, a, which, first, s_sem, r_sem):
+            out_u[a, j, :, part] = piece.reshape(cells_x, kc, cells_y)
+        send_back(step, a, j, 1, (1 - here) * group, cs_sem, cr_sem)
+        send_back(step, a, j, 0, base, os_sem, or_sem)
+
+    def send_back(step, a, j, which, first, s_sem, r_sem):
         def send(k, carry):
             to = lax.rem(seat + k, group)
             remote(
-                out_u.at[a, first + to], in_u.at[a, which, seat], s_sem.at[step, a], r_sem.at[step, a], base + to
+                out_u.at[a, j, first + to], in_u.at[a, which, j, seat], s_sem.at[step, a, j], r_sem.at[step, a, j],
+                base + to,
             ).start()
             return carry
 
         lax.fori_loop(1, group, send, 0)
-        in_u[a, which, seat] = out_u[a, first + seat]
+        in_u[a, which, j, seat] = out_u[a, j, first + seat]
 
     def inverse_z(a, which):
-        total = None
-        for part in range(2):
-            field = in_u[a, which, :, part].reshape(kz_half, cells_y)
-            dims = (((0,), (0,)), ((), ()))
-            term = three_pass(split(field), (vz_h[here, part], vz_l[here, part]), dims)
-            total = term if total is None else total + term
-        return total
+        field = in_u[a, which].reshape(chunks * group * 2 * kc, cells_y)
+        return three_pass(split(field), (vz_h[here], vz_l[here]), (((0,), (0,)), ((), ())))
 
     def send_part(step, a):
-        drain(in_u.at[a, 1, pl.ds(0, group - 1)], cr_sem.at[step, a])
+        for j in range(chunks):
+            drain(in_u.at[a, 1, j, pl.ds(0, group - 1)], cr_sem.at[step, a, j])
         part_out[a] = inverse_z(a, 1)
         remote(part_out.at[a], part_in.at[a], ps_sem.at[step, a], pr_sem.at[step, a], twin).start()
 
+    loads[1].wait()
     for step in range(MATVECS):
         source, image = (pol_ref, first_ref) if step == 0 else (first_ref, second_ref)
         if step == 0:
             pl.semaphore_wait(barrier, group)
             for c in range(3):
                 send_raw(step, c, source[c, 0] * mask_ref[...])
+            for load in loads[2:]:
+                load.wait()
             for c in range(3):
-                forward_z(step, c, 0, raw_out[c])
+                forward_z(c, 0, raw_out[c])
+                send_block(step, c, 0, 0)
+            for j in range(1, chunks):
+                for c in range(3):
+                    send_block(step, c, 0, j)
             order_green()
         for c in range(3):
             drain(raw_in.at[c], wr_sem.at[step, c])
-            forward_z(step, c, 1, raw_in[c])
-            if c > 0:
-                forward_yx(step, c - 1)
-        forward_yx(step, 2)
-        for a in range(3):
-            backward_xy(step, a)
-            if a > 0:
-                send_part(step, a - 1)
+            forward_z(c, 1, raw_in[c])
+            send_block(step, c, 1, 0)
+        for j in range(1, chunks):
+            for c in range(3):
+                send_block(step, c, 1, j)
+        for j in range(chunks):
+            for c in range(3):
+                forward_yx(step, c, j)
+            for a in range(3):
+                backward_xy(step, a, j)
+                if j == chunks - 1 and a > 0:
+                    send_part(step, a - 1)
         send_part(step, 2)
         for c in range(3):
             drain(raw_out.at[c], ws_sem.at[step, c])
-            drain(in_t.at[c, pl.ds(0, n - 2)], ts_sem.at[step, c])
+            for j in range(chunks):
+                drain(in_t.at[c, j, pl.ds(0, n - 2)], ts_sem.at[step, c, j])
         for a in range(3):
-            drain(in_u.at[a, 0, pl.ds(0, group - 1)], or_sem.at[step, a])
+            for j in range(chunks):
+                drain(in_u.at[a, 0, j, pl.ds(0, group - 1)], or_sem.at[step, a, j])
             own = inverse_z(a, 0)
             masked = source[a, 0] * mask_ref[...]
             drain(part_in.at[a], pr_sem.at[step, a])
             image[a, 0] = inv_ref[0] * masked - mask_ref[...] * (own + part_in[a])
             if step + 1 < MATVECS:
                 send_raw(step + 1, a, image[a, 0] * mask_ref[...])
-                forward_z(step + 1, a, 0, raw_out[a])
+                forward_z(a, 0, raw_out[a])
+                for j in range(chunks):
+                    send_block(step + 1, a, 0, j)
         for a in range(3):
-            drain(in_u.at[a, 1, pl.ds(0, group - 1)], cs_sem.at[step, a])
-            drain(in_u.at[a, 0, pl.ds(0, group - 1)], os_sem.at[step, a])
+            for j in range(chunks):
+                drain(in_u.at[a, 1, j, pl.ds(0, group - 1)], cs_sem.at[step, a, j])
+                drain(in_u.at[a, 0, j, pl.ds(0, group - 1)], os_sem.at[step, a, j])
             drain(part_out.at[a], ps_sem.at[step, a])
 
 
@@ -305,43 +328,56 @@
     kc = min(8, kz_own)
     chunks = kz_own // kc
     halves = padded_y // 128
+    group = n // 2
+
+    def by_block(table):
+        table = table.reshape(2, 2, group, chunks, kc, cells_z)
+        return table.transpose(1, 3, 2, 0, 4, 5).reshape(2, chunks * group * 2 * kc, cells_z)
+
     cos, sin = tables(padded_z, cells_z, padded_z)
-    wz = split_table(np.stack([cos, -sin]).reshape(2, 2, cells_z, cells_z).swapaxes(0, 1))
+    wz = split_table(by_block(np.stack([cos, -sin])))
+    vz = split_table(by_block(np.stack([cos, -sin])) / (padded_x * padded_y * padded_z))
     cos, sin = tables(cells_y, padded_y, padded_y)
     wy = split_table(np.block([[cos, -sin], [sin, cos]]))
     cos, sin = tables(padded_y, cells_y, padded_y)
     vy = split_table(np.block([[cos, sin], [-sin, cos]]))
-    cos, sin = tables(padded_z, cells_z, padded_z)
-    vz = np.stack([cos, -sin]).reshape(2, 2, cells_z, cells_z).swapaxes(0, 1)
-    vz = split_table(vz / (padded_x * padded_y * padded_z))
+    constants = [jnp.asarray(table) for table in wz + wy + vy + vz]
+    anywhere = pl.BlockSpec(memory_space=pl.ANY)
     vmem = pl.BlockSpec(memory_space=pltpu.VMEM)
+    dma = pltpu.SemaphoreType.DMA
     images = pl.pallas_call(
         functools.partial(kernel, n, cells_x, padded_x, kz_own, kc),
         out_shape=(jax.ShapeDtypeStruct(polarization.shape, F32),) * 2,
-        in_specs=[vmem] * 3 + [pl.BlockSpec(memory_space=pl.ANY)] + [vmem] * 8,
+        in_specs=[anywhere] * 12,
         out_specs=(vmem, vmem),
         scratch_shapes=[
+            pltpu.VMEM(polarization.shape, F32),
+            pltpu.VMEM(inverse_polarizability.shape, F32),
+            pltpu.VMEM(occupancy.shape, jnp.int32),
+            *[pltpu.VMEM(table.shape, BF16) for table in constants],
             pltpu.VMEM(green_fourier.shape, F32),
             pltpu.VMEM((chunks * halves, 6, padded_x, kc, 128), F32),
             pltpu.VMEM((cells_y, cells_z), F32),
             pltpu.VMEM((3, cells_y, cells_z), F32),
             pltpu.VMEM((3, cells_y, cells_z), F32),
-            pltpu.VMEM((3, 2, n // 2, 2, kz_own, cells_y), F32),
-            pltpu.VMEM((3, n, 2, kz_own, cells_y), F32),
+            pltpu.VMEM((3, 2, chunks, group, 2, kc, cells_y), F32),
+            pltpu.VMEM((3, chunks, n, 2, kc, cells_y), F32),
             pltpu.VMEM((chunks * halves, 2, cells_x, kc, 128), F32),
             pltpu.VMEM((chunks * halves, 6, padded_x, kc, 128), F32),
-            pltpu.VMEM((3, n, 2, kz_own, cells_y), F32),
-            pltpu.VMEM((3, 2, n // 2, 2, kz_own, cells_y), F32),
+            pltpu.VMEM((3, chunks, n, 2, kc, cells_y), F32),
+            pltpu.VMEM((3, 2, chunks, group, 2, kc, cells_y), F32),
             pltpu.VMEM((3, cells_y, cells_z), F32),
             pltpu.VMEM((3, cells_y, cells_z), F32),
-            pltpu.SemaphoreType.DMA,
-            *[pltpu.SemaphoreType.DMA((MATVECS, 3))] * 10,
+            dma,
+            dma((11,)),
+            *[dma((MATVECS, 3))] * 2,
+            *[dma((MATVECS, 3, chunks))] * 6,
+            *[dma((MATVECS, 3))] * 2,
         ],
         compiler_params=pltpu.CompilerParams(
             collective_id=0, has_side_effects=True, vmem_limit_bytes=60 * 1024 * 1024
         ),
-    )(polarization, inverse_polarizability, occupancy, green_fourier, *map(jnp.asarray, wz + wy + vy + vz))
-    anywhere = pl.BlockSpec(memory_space=pl.ANY)
+    )(polarization, inverse_polarizability, occupancy, green_fourier, *constants)
     return pl.pallas_call(
         deliver,
         out_shape=(jax.ShapeDtypeStruct(polarization.shape, F32),) * 2,

time: 76.5 us -> 73.2 us (0.957)
  Pallas kernels: 75.7 us -> 72.4 us
    pallas_call x1, Pallas kernels: 73.9 us -> 70.6 us  [per_device(): pl.pallas_call(functools.partial(kernel, n, cells_x, padded_x, kz_own, kc...]
where the time goes in v1:
time: 73.2 us; the launch traced here: 73 us
  Pallas kernels  72.4 us (99%)
    pallas_call x1, Pallas kernels, per_device(): pl.pallas_call(functools.partial(kernel, n, cells_x, padded_x, kz_own, kc...  70.6 us
    pallas_call x1, Pallas kernels, per_device(): pl.pallas_call(deliver, out_shape=(jax.ShapeDtypeStruct(polarization.shap...  1.73 us

profile of v1, /device:TPU:0, one launch (start us, length us, event | category | flops | bytes accessed | tf_op | source)
XLA Modules:
  0.0 73.0 jit_solution(7219112427237044882)
XLA Ops:
  0.6 70.6 %shard_map.131 = (f32[3,1,128,128]{3,2,1,0:T(8,128)}, f32[3,1,128,128]{3,2,1,0:T(8,128)}) custom-call(f32[3,1,128,128]{3,2,1,0:T(8,128)} %pol_hbm.1, f32[1,128,128]{2,1,0:T(8,128)} %inv_hbm.1, s32[1,16,16]{2,1,0:T(8,128)} %occ_hbm.1, f32[6,16,32,256]{3,2,1,0:T(8,128)} %green_ref.1, bf16[2,256,128]{2,1,0:T(8,128)(2,1)} %constant.16.clone.refs_0_, ...), custom_call_target="tpu_custom_call" | custom-call | tf_op jit(solution)/shard_map/pallas_call | solution.py:348
  71.3 1.7 %shard_map.132 = (f32[3,1,128,128]{3,2,1,0:T(8,128)}, f32[3,1,128,128]{3,2,1,0:T(8,128)}) custom-call(f32[3,1,128,128]{3,2,1,0:T(8,128)} %get-tuple-element.4.first_ref, f32[3,1,128,128]{3,2,1,0:T(8,128)} %get-tuple-element.5.second_ref), custom_call_target="tpu_custom_call" | custom-call | tf_op jit(solution)/shard_map/pallas_call | solution.py:381

commit v2 on v1

--- a/solution.py
+++ b/solution.py
@@ -302,19 +302,12 @@
             drain(part_out.at[a], ps_sem.at[step, a])
 
 
-def deliver(first_ref, second_ref, first_out, second_out, first, second, in_sem, out_sem):
-    loads = [
-        pltpu.make_async_copy(source, held, in_sem.at[i])
-        for i, (source, held) in enumerate(((first_ref, first), (second_ref, second)))
-    ]
+def deliver(first, second, first_out, second_out, out_sem):
     stores = [
         pltpu.make_async_copy(held, target, out_sem.at[i])
         for i, (held, target) in enumerate(((first, first_out), (second, second_out)))
     ]
-    for copy in loads:
-        copy.start()
-    for load, store in zip(loads, stores):
-        load.wait()
+    for store in stores:
         store.start()
     for store in stores:
         store.wait()
@@ -347,7 +340,7 @@
     dma = pltpu.SemaphoreType.DMA
     images = pl.pallas_call(
         functools.partial(kernel, n, cells_x, padded_x, kz_own, kc),
-        out_shape=(jax.ShapeDtypeStruct(polarization.shape, F32),) * 2,
+        out_shape=(pltpu.VMEM(polarization.shape, F32),) * 2,
         in_specs=[anywhere] * 12,
         out_specs=(vmem, vmem),
         scratch_shapes=[
@@ -381,10 +374,10 @@
     return pl.pallas_call(
         deliver,
         out_shape=(jax.ShapeDtypeStruct(polarization.shape, F32),) * 2,
-        in_specs=[anywhere] * 2,
+        in_specs=[vmem] * 2,
         out_specs=(anywhere, anywhere),
-        scratch_shapes=[pltpu.VMEM(polarization.shape, F32)] * 2 + [pltpu.SemaphoreType.DMA((2,))] * 2,
-    )(*images)
+        scratch_shapes=[dma((2,))],
+    )(*[pltpu.with_memory_space_constraint(x, pltpu.VMEM) for x in images])
 
 
 def solution(mesh):

time: 73.2 us -> 71.3 us (0.974)
  Pallas kernels: 72.4 us -> 70.5 us
    pallas_call x1, Pallas kernels: 1.73 us -> 0.76 us  [per_device(): pl.pallas_call(deliver, out_shape=(jax.ShapeDtypeStruct(polarization.shap...]
    pallas_call x1, Pallas kernels: 70.6 us -> 69.8 us  [per_device(): pl.pallas_call(functools.partial(kernel, n, cells_x, padded_x, kz_own, kc...]
where the time goes in v2:
time: 71.3 us; the launch traced here: 71.2 us
  Pallas kernels  70.5 us (99%)
    pallas_call x1, Pallas kernels, per_device(): pl.pallas_call(functools.partial(kernel, n, cells_x, padded_x, kz_own, kc...  69.8 us

profile of v2, /device:TPU:0, one launch (start us, length us, event | category | flops | bytes accessed | tf_op | source)
XLA Modules:
  0.0 71.2 jit_solution(1232928478208877550)
XLA Ops:
  0.6 69.8 %shard_map.131 = (f32[3,1,128,128]{3,2,1,0:T(8,128)S(1)}, f32[3,1,128,128]{3,2,1,0:T(8,128)S(1)}) custom-call(f32[3,1,128,128]{3,2,1,0:T(8,128)} %pol_hbm.1, f32[1,128,128]{2,1,0:T(8,128)} %inv_hbm.1, s32[1,16,16]{2,1,0:T(8,128)} %occ_hbm.1, f32[6,16,32,256]{3,2,1,0:T(8,128)} %green_ref.1, bf16[2,256,128]{2,1,0:T(8,128)(2,1)} %constant.16.clone.refs_0_, ...), custom_call_target="tpu_custom_call" | custom-call | tf_op jit(solution)/shard_map/pallas_call | solution.py:341
  70.4 0.8 %shard_map.132 = (f32[3,1,128,128]{3,2,1,0:T(8,128)}, f32[3,1,128,128]{3,2,1,0:T(8,128)}) custom-call(f32[3,1,128,128]{3,2,1,0:T(8,128)S(1)} %get-tuple-element.4.first, f32[3,1,128,128]{3,2,1,0:T(8,128)S(1)} %get-tuple-element.5.second), custom_call_target="tpu_custom_call" | custom-call | tf_op jit(solution)/shard_map/pallas_call | solution.py:374

commit v3 on v2

--- a/solution.py
+++ b/solution.py
@@ -11,6 +11,7 @@
 
 BLOCK = 8
 MATVECS = 2
+SPLIT = 1
 F32 = jnp.float32
 BF16 = jnp.bfloat16
 COMBOS = ((0, 3, 4), (3, 1, 5), (4, 5, 2))
@@ -73,7 +74,7 @@
 
 
 def kernel(
-    n, cells_x, padded_x, kz_own, kc,
+    n, cells_x, padded_x, kz_own, kx, kc,
     pol_hbm, inv_hbm, occ_hbm, green_ref, *refs,
 ):
     tables_hbm, refs = refs[:8], refs[8:]
@@ -88,9 +89,14 @@
     group = n // 2
     here = me // group
     seat = lax.rem(me, group)
-    twin = lax.rem(me + group, n)
+    plane = n // 4
+
+    def twin_of(device):
+        return n - plane - device + 2 * lax.rem(device, plane)
+
+    twin = twin_of(me)
     base = here * group
-    chunks = kz_own // kc
+    chunks, sub = kz_own // kx, kx // kc
     cells_y, cells_z = mask_ref.shape
     padded_y = 2 * cells_y
     halves = padded_y // 128
@@ -136,7 +142,7 @@
         green_copy.wait()
 
         def one(g, carry):
-            for j in range(chunks):
+            for j in range(chunks * sub):
                 for t in range(0, padded_x, 8):
                     tile = green_raw[g, j * kc:(j + 1) * kc, t:t + 8, :]
                     tile = jnp.swapaxes(tile, 0, 1)
@@ -153,7 +159,7 @@
     def forward_z(c, which, field):
         dims = (((1,), (1,)), ((), ()))
         res = three_pass((wz_h[here], wz_l[here]), split(field), dims)
-        out_t[c, which] = res.reshape(chunks, group, 2, kc, cells_y)
+        out_t[c, which] = res.reshape(chunks, group, 2, kx, cells_y)
 
     def send_block(step, c, which, j):
         slab = me if which == 0 else twin
@@ -173,16 +179,18 @@
 
     def forward_yx(step, c, j):
         drain(in_t.at[c, j, pl.ds(0, n - 2)], tr_sem.at[step, c, j])
-        parts = [in_t[c, j, :, part].reshape(cells_x * kc, cells_y) for part in range(2)]
+        parts = [in_t[c, j, :, part].reshape(cells_x * kx, cells_y) for part in range(2)]
         dims = (((1,), (0,)), ((), ()))
         res = three_pass(split(jnp.concatenate(parts, axis=1)), (wy_h[...], wy_l[...]), dims)
         for part in range(2):
             for h in range(halves):
                 at = part * padded_y + h * 128
-                lines[j * halves + h, part] = res[:, at:at + 128].reshape(cells_x, kc, 128)
+                piece = res[:, at:at + 128].reshape(cells_x, kx, 128)
+                for p in range(sub):
+                    lines[(j * sub + p) * halves + h, part] = piece[:, p * kc:(p + 1) * kc]
 
         def columns(h, carry):
-            i = j * halves + h
+            i = j * sub * halves + h
             line = [(lines[i, 0, x], lines[i, 1, x]) for x in range(cells_x)]
             for m, (re, im) in enumerate(fft(line, -1)):
                 spec[i, 2 * c, 2 * m], spec[i, 2 * c + 1, 2 * m] = re, im
@@ -191,13 +199,13 @@
                 spec[i, 2 * c, 2 * m + 1], spec[i, 2 * c + 1, 2 * m + 1] = re, im
             return carry
 
-        lax.fori_loop(0, halves, columns, 0)
+        lax.fori_loop(0, sub * halves, columns, 0)
 
     def backward_xy(step, a, j):
         row = COMBOS[a]
 
         def columns(h, carry):
-            i = j * halves + h
+            i = j * sub * halves + h
 
             def field(k):
                 g = [green[i, r, k] for r in row]
@@ -214,32 +222,35 @@
                 lines[i, 1, x] += im
             return carry
 
-        lax.fori_loop(0, halves, columns, 0)
-        parts = [
-            lines[j * halves + h, part].reshape(cells_x * kc, 128) for part in range(2) for h in range(halves)
-        ]
+        lax.fori_loop(0, sub * halves, columns, 0)
+        parts = []
+        for part in range(2):
+            for h in range(halves):
+                pieces = [lines[(j * sub + p) * halves + h, part] for p in range(sub)]
+                piece = pieces[0] if sub == 1 else jnp.concatenate(pieces, axis=1)
+                parts.append(piece.reshape(cells_x * kx, 128))
         dims = (((1,), (0,)), ((), ()))
         res = three_pass(split(jnp.concatenate(parts, axis=1)), (vy_h[...], vy_l[...]), dims)
         for part in range(2):
             piece = res[:, part * cells_y:(part + 1) * cells_y]
-            out_u[a, j, :, part] = piece.reshape(cells_x, kc, cells_y)
-        send_back(step, a, j, 1, (1 - here) * group, cs_sem, cr_sem)
-        send_back(step, a, j, 0, base, os_sem, or_sem)
-
-    def send_back(step, a, j, which, first, s_sem, r_sem):
+            out_u[a, j, :, part] = piece.reshape(cells_x, kx, cells_y)
+        send_back(step, a, j, 1, twin_of, cs_sem, cr_sem)
+        send_back(step, a, j, 0, lambda device: device, os_sem, or_sem)
+
+    def send_back(step, a, j, which, slab_of, s_sem, r_sem):
         def send(k, carry):
             to = lax.rem(seat + k, group)
             remote(
-                out_u.at[a, j, first + to], in_u.at[a, which, j, seat], s_sem.at[step, a, j], r_sem.at[step, a, j],
+                out_u.at[a, j, slab_of(base + to)], in_u.at[a, which, j, seat], s_sem.at[step, a, j], r_sem.at[step, a, j],
                 base + to,
             ).start()
             return carry
 
         lax.fori_loop(1, group, send, 0)
-        in_u[a, which, j, seat] = out_u[a, j, first + seat]
+        in_u[a, which, j, seat] = out_u[a, j, slab_of(me)]
 
     def inverse_z(a, which):
-        field = in_u[a, which].reshape(chunks * group * 2 * kc, cells_y)
+        field = in_u[a, which].reshape(chunks * group * 2 * kx, cells_y)
         return three_pass(split(field), (vz_h[here], vz_l[here]), (((0,), (0,)), ((), ())))
 
     def send_part(step, a):
@@ -318,14 +329,15 @@
     _, kz_own, padded_x, padded_y = green_fourier.shape
     padded_z = 2 * cells_z
     cells_x = padded_x // 2
-    kc = min(8, kz_own)
-    chunks = kz_own // kc
+    kx = kz_own // SPLIT if kz_own % (8 * SPLIT) == 0 else kz_own
+    kc = min(8, kx)
+    chunks = kz_own // kx
     halves = padded_y // 128
     group = n // 2
 
     def by_block(table):
-        table = table.reshape(2, 2, group, chunks, kc, cells_z)
-        return table.transpose(1, 3, 2, 0, 4, 5).reshape(2, chunks * group * 2 * kc, cells_z)
+        table = table.reshape(2, 2, group, chunks, kx, cells_z)
+        return table.transpose(1, 3, 2, 0, 4, 5).reshape(2, chunks * group * 2 * kx, cells_z)
 
     cos, sin = tables(padded_z, cells_z, padded_z)
     wz = split_table(by_block(np.stack([cos, -sin])))
@@ -339,7 +351,7 @@
     vmem = pl.BlockSpec(memory_space=pltpu.VMEM)
     dma = pltpu.SemaphoreType.DMA
     images = pl.pallas_call(
-        functools.partial(kernel, n, cells_x, padded_x, kz_own, kc),
+        functools.partial(kernel, n, cells_x, padded_x, kz_own, kx, kc),
         out_shape=(pltpu.VMEM(polarization.shape, F32),) * 2,
         in_specs=[anywhere] * 12,
         out_specs=(vmem, vmem),
@@ -349,16 +361,16 @@
             pltpu.VMEM(occupancy.shape, jnp.int32),
             *[pltpu.VMEM(table.shape, BF16) for table in constants],
             pltpu.VMEM(green_fourier.shape, F32),
-            pltpu.VMEM((chunks * halves, 6, padded_x, kc, 128), F32),
+            pltpu.VMEM((kz_own // kc * halves, 6, padded_x, kc, 128), F32),
             pltpu.VMEM((cells_y, cells_z), F32),
             pltpu.VMEM((3, cells_y, cells_z), F32),
             pltpu.VMEM((3, cells_y, cells_z), F32),
-            pltpu.VMEM((3, 2, chunks, group, 2, kc, cells_y), F32),
-            pltpu.VMEM((3, chunks, n, 2, kc, cells_y), F32),
-            pltpu.VMEM((chunks * halves, 2, cells_x, kc, 128), F32),
-            pltpu.VMEM((chunks * halves, 6, padded_x, kc, 128), F32),
-            pltpu.VMEM((3, chunks, n, 2, kc, cells_y), F32),
-            pltpu.VMEM((3, 2, chunks, group, 2, kc, cells_y), F32),
+            pltpu.VMEM((3, 2, chunks, group, 2, kx, cells_y), F32),
+            pltpu.VMEM((3, chunks, n, 2, kx, cells_y), F32),
+            pltpu.VMEM((kz_own // kc * halves, 2, cells_x, kc, 128), F32),
+            pltpu.VMEM((kz_own // kc * halves, 6, padded_x, kc, 128), F32),
+            pltpu.VMEM((3, chunks, n, 2, kx, cells_y), F32),
+            pltpu.VMEM((3, 2, chunks, group, 2, kx, cells_y), F32),
             pltpu.VMEM((3, cells_y, cells_z), F32),
             pltpu.VMEM((3, cells_y, cells_z), F32),
             dma,

time: 71.3 us -> 68.6 us (0.962)
  Pallas kernels: 70.5 us -> 67.8 us
    pallas_call x1, Pallas kernels: 69.8 us -> 67 us  [per_device(): pl.pallas_call(functools.partial(kernel, n, cells_x, padded_x, kz_own, kx...]
where the time goes in v3:
time: 68.6 us; the launch traced here: 68.4 us
  Pallas kernels  67.8 us (99%)
    pallas_call x1, Pallas kernels, per_device(): pl.pallas_call(functools.partial(kernel, n, cells_x, padded_x, kz_own, kx...  67 us

profile of v3, /device:TPU:0, one launch (start us, length us, event | category | flops | bytes accessed | tf_op | source)
XLA Modules:
  0.0 68.4 jit_solution(11225124184662714467)
XLA Ops:
  0.6 67.0 %shard_map.131 = (f32[3,1,128,128]{3,2,1,0:T(8,128)S(1)}, f32[3,1,128,128]{3,2,1,0:T(8,128)S(1)}) custom-call(f32[3,1,128,128]{3,2,1,0:T(8,128)} %pol_hbm.1, f32[1,128,128]{2,1,0:T(8,128)} %inv_hbm.1, s32[1,16,16]{2,1,0:T(8,128)} %occ_hbm.1, f32[6,16,32,256]{3,2,1,0:T(8,128)} %green_ref.1, bf16[2,256,128]{2,1,0:T(8,128)(2,1)} %constant.16.clone.refs_0_, ...), custom_call_target="tpu_custom_call" | custom-call | tf_op jit(solution)/shard_map/pallas_call | solution.py:353
  67.7 0.8 %shard_map.132 = (f32[3,1,128,128]{3,2,1,0:T(8,128)}, f32[3,1,128,128]{3,2,1,0:T(8,128)}) custom-call(f32[3,1,128,128]{3,2,1,0:T(8,128)S(1)} %get-tuple-element.4.first, f32[3,1,128,128]{3,2,1,0:T(8,128)S(1)} %get-tuple-element.5.second), custom_call_target="tpu_custom_call" | custom-call | tf_op jit(solution)/shard_map/pallas_call | solution.py:386

commit v4 on v3

--- a/solution.py
+++ b/solution.py
@@ -12,6 +12,7 @@
 BLOCK = 8
 MATVECS = 2
 SPLIT = 1
+STAGGER_NS = 3000
 F32 = jnp.float32
 BF16 = jnp.bfloat16
 COMBOS = ((0, 3, 4), (3, 1, 5), (4, 5, 2))
@@ -235,7 +236,6 @@
             piece = res[:, part * cells_y:(part + 1) * cells_y]
             out_u[a, j, :, part] = piece.reshape(cells_x, kx, cells_y)
         send_back(step, a, j, 1, twin_of, cs_sem, cr_sem)
-        send_back(step, a, j, 0, lambda device: device, os_sem, or_sem)
 
     def send_back(step, a, j, which, slab_of, s_sem, r_sem):
         def send(k, carry):
@@ -249,6 +249,10 @@
         lax.fori_loop(1, group, send, 0)
         in_u[a, which, j, seat] = out_u[a, j, slab_of(me)]
 
+    def send_home(step, a):
+        for j in range(chunks):
+            send_back(step, a, j, 0, lambda device: device, os_sem, or_sem)
+
     def inverse_z(a, which):
         field = in_u[a, which].reshape(chunks * group * 2 * kx, cells_y)
         return three_pass(split(field), (vz_h[here], vz_l[here]), (((0,), (0,)), ((), ())))
@@ -264,6 +268,7 @@
         source, image = (pol_ref, first_ref) if step == 0 else (first_ref, second_ref)
         if step == 0:
             pl.semaphore_wait(barrier, group)
+            pl.delay((1 - lax.axis_index("comp")) * STAGGER_NS)
             for c in range(3):
                 send_raw(step, c, source[c, 0] * mask_ref[...])
             for load in loads[2:]:
@@ -288,8 +293,11 @@
             for a in range(3):
                 backward_xy(step, a, j)
                 if j == chunks - 1 and a > 0:
-                    send_part(step, a - 1)
-        send_part(step, 2)
+                    send_home(step, a - 1)
+        for a in range(3):
+            send_part(step, a)
+            if a == 0:
+                send_home(step, 2)
         for c in range(3):
             drain(raw_out.at[c], ws_sem.at[step, c])
             for j in range(chunks):

time: 68.6 us -> 66 us (0.962)
  Pallas kernels: 67.8 us -> 65.1 us
    pallas_call x1, Pallas kernels: 67 us -> 64.4 us  [per_device(): pl.pallas_call(functools.partial(kernel, n, cells_x, padded_x, kz_own, kx...]
where the time goes in v4:
time: 66 us; the launch traced here: 65.8 us
  Pallas kernels  65.1 us (99%)
    pallas_call x1, Pallas kernels, per_device(): pl.pallas_call(functools.partial(kernel, n, cells_x, padded_x, kz_own, kx...  64.4 us

profile of v4, /device:TPU:0, one launch (start us, length us, event | category | flops | bytes accessed | tf_op | source)
XLA Modules:
  0.0 65.8 jit_solution(10501888015670598146)
XLA Ops:
  0.6 64.4 %shard_map.131 = (f32[3,1,128,128]{3,2,1,0:T(8,128)S(1)}, f32[3,1,128,128]{3,2,1,0:T(8,128)S(1)}) custom-call(f32[3,1,128,128]{3,2,1,0:T(8,128)} %pol_hbm.1, f32[1,128,128]{2,1,0:T(8,128)} %inv_hbm.1, s32[1,16,16]{2,1,0:T(8,128)} %occ_hbm.1, f32[6,16,32,256]{3,2,1,0:T(8,128)} %green_ref.1, bf16[2,256,128]{2,1,0:T(8,128)(2,1)} %constant.16.clone.refs_0_, ...), custom_call_target="tpu_custom_call" | custom-call | tf_op jit(solution)/shard_map/pallas_call | solution.py:361
  65.0 0.8 %shard_map.132 = (f32[3,1,128,128]{3,2,1,0:T(8,128)}, f32[3,1,128,128]{3,2,1,0:T(8,128)}) custom-call(f32[3,1,128,128]{3,2,1,0:T(8,128)S(1)} %get-tuple-element.4.first, f32[3,1,128,128]{3,2,1,0:T(8,128)S(1)} %get-tuple-element.5.second), custom_call_target="tpu_custom_call" | custom-call | tf_op jit(solution)/shard_map/pallas_call | solution.py:394

commit v5 on v4

--- a/solution.py
+++ b/solution.py
@@ -166,7 +166,7 @@
         slab = me if which == 0 else twin
 
         def send(k, carry):
-            to = lax.rem(seat + k, group)
+            to = seat ^ (group - k)
             remote(
                 out_t.at[c, which, j, to], in_t.at[c, j, slab], ts_sem.at[step, c, j], tr_sem.at[step, c, j], base + to
             ).start()
@@ -239,7 +239,7 @@
 
     def send_back(step, a, j, which, slab_of, s_sem, r_sem):
         def send(k, carry):
-            to = lax.rem(seat + k, group)
+            to = seat ^ (group - k)
             remote(
                 out_u.at[a, j, slab_of(base + to)], in_u.at[a, which, j, seat], s_sem.at[step, a, j], r_sem.at[step, a, j],
                 base + to,

time: 66 us -> 65.2 us (0.988)
  Pallas kernels: 65.1 us -> 64.3 us
    pallas_call x1, Pallas kernels: 64.4 us -> 63.6 us  [per_device(): pl.pallas_call(functools.partial(kernel, n, cells_x, padded_x, kz_own, kx...]
where the time goes in v5:
time: 65.2 us; the launch traced here: 65 us
  Pallas kernels  64.3 us (99%)
    pallas_call x1, Pallas kernels, per_device(): pl.pallas_call(functools.partial(kernel, n, cells_x, padded_x, kz_own, kx...  63.6 us

profile of v5, /device:TPU:0, one launch (start us, length us, event | category | flops | bytes accessed | tf_op | source)
XLA Modules:
  0.0 65.0 jit_solution(5935486153946914136)
XLA Ops:
  0.6 63.6 %shard_map.131 = (f32[3,1,128,128]{3,2,1,0:T(8,128)S(1)}, f32[3,1,128,128]{3,2,1,0:T(8,128)S(1)}) custom-call(f32[3,1,128,128]{3,2,1,0:T(8,128)} %pol_hbm.1, f32[1,128,128]{2,1,0:T(8,128)} %inv_hbm.1, s32[1,16,16]{2,1,0:T(8,128)} %occ_hbm.1, f32[6,16,32,256]{3,2,1,0:T(8,128)} %green_ref.1, bf16[2,256,128]{2,1,0:T(8,128)(2,1)} %constant.16.clone.refs_0_, ...), custom_call_target="tpu_custom_call" | custom-call | tf_op jit(solution)/shard_map/pallas_call | solution.py:361
  64.2 0.8 %shard_map.132 = (f32[3,1,128,128]{3,2,1,0:T(8,128)}, f32[3,1,128,128]{3,2,1,0:T(8,128)}) custom-call(f32[3,1,128,128]{3,2,1,0:T(8,128)S(1)} %get-tuple-element.4.first, f32[3,1,128,128]{3,2,1,0:T(8,128)S(1)} %get-tuple-element.5.second), custom_call_target="tpu_custom_call" | custom-call | tf_op jit(solution)/shard_map/pallas_call | solution.py:394

commit v6 on v5

--- a/solution.py
+++ b/solution.py
@@ -12,7 +12,7 @@
 BLOCK = 8
 MATVECS = 2
 SPLIT = 1
-STAGGER_NS = 3000
+STAGGER_NS = 3500
 F32 = jnp.float32
 BF16 = jnp.bfloat16
 COMBOS = ((0, 3, 4), (3, 1, 5), (4, 5, 2))

time: 65.2 us -> 65.2 us (level)
  no operation moved by 1% of the time
where the time goes in v6:
time: 65.2 us; the launch traced here: 65 us
  Pallas kernels  64.3 us (99%)
    pallas_call x1, Pallas kernels, per_device(): pl.pallas_call(functools.partial(kernel, n, cells_x, padded_x, kz_own, kx...  63.6 us

profile of v6, /device:TPU:0, one launch (start us, length us, event | category | flops | bytes accessed | tf_op | source)
XLA Modules:
  0.0 65.0 jit_solution(10192711160709698824)
XLA Ops:
  0.6 63.6 %shard_map.131 = (f32[3,1,128,128]{3,2,1,0:T(8,128)S(1)}, f32[3,1,128,128]{3,2,1,0:T(8,128)S(1)}) custom-call(f32[3,1,128,128]{3,2,1,0:T(8,128)} %pol_hbm.1, f32[1,128,128]{2,1,0:T(8,128)} %inv_hbm.1, s32[1,16,16]{2,1,0:T(8,128)} %occ_hbm.1, f32[6,16,32,256]{3,2,1,0:T(8,128)} %green_ref.1, bf16[2,256,128]{2,1,0:T(8,128)(2,1)} %constant.16.clone.refs_0_, ...), custom_call_target="tpu_custom_call" | custom-call | tf_op jit(solution)/shard_map/pallas_call | solution.py:361
  64.2 0.8 %shard_map.132 = (f32[3,1,128,128]{3,2,1,0:T(8,128)}, f32[3,1,128,128]{3,2,1,0:T(8,128)}) custom-call(f32[3,1,128,128]{3,2,1,0:T(8,128)S(1)} %get-tuple-element.4.first, f32[3,1,128,128]{3,2,1,0:T(8,128)S(1)} %get-tuple-element.5.second), custom_call_target="tpu_custom_call" | custom-call | tf_op jit(solution)/shard_map/pallas_call | solution.py:394
